TPU v7x, 32 devices: a whole 2x2x4 slice. The times are simulated.
32 devices in a mesh: src: 8 (over z, core), tgt: 4 (over y, x).
Axes of the slice: x: 2, y: 2, z: 4, core: 2. Of those that a mesh axis runs over, the one named last changes fastest.
Arguments:
- source_embed: bfloat16 [128, 128, 128], P('src', None, 'tgt'), may hold values from -4 to 4
- target_embed: bfloat16 [64, 128, 128], P('tgt', None, 'src'), may hold values from -4 to 4
- source_mass: float32 [128, 128], P('src'), may hold values from 10 to 14
- target_mass: float32 [64, 128], P('tgt'), may hold values from 10 to 14
- target_start: float32 [64, 128], P('tgt'), may hold values from -6 to 6
- block_pairs: int32 [8, 4, 128, 2], P('src', 'tgt'), may hold values from 0 to 15, as said below
- counts: int32 [8, 4], P('src', 'tgt'), may hold values from 16 to 128, as said below
Outputs:
- sender_log_scaling: float32 [128, 128], P('src')
- target_dual_potential: float32 [64, 128], P('tgt')
Inputs may be any that keep to these rules, and one draw needn't show every extreme that they name: `block_pairs`: entry 0 of a slot is a local source block (below 16), entry 1 a local target block (below 16). The live slots of a device name distinct pairs; its first 16 slots name each of its target blocks once and each of its source blocks at least once. Slots at or past the device's count are not kept and hold arbitrary block numbers. `counts`: some device has all 128 slots live in every draw.
All inputs are finite; a program needn't handle non-finite values.
Results may differ from a plain program's by a relative error of at most 0.0003.
Values may be sent and summed in bfloat16 or wider, within the bound.
A program may use at most 64 MiB of HBM per device.

v0:
```python
import jax
import jax.numpy as jnp
from jax import lax
from jax.sharding import PartitionSpec as P

ITERS = 2
smoothing_epsilon = 4.0
empty_peak = -1e30
slot_batch = 8


def from_partner(block, axis, bit):
    count = lax.axis_size(axis)
    route = []
    for low in range(count):
        high = low | 1 << bit
        if high != low and high < count:
            route += [(low, high), (high, low)]
    return lax.ppermute(block, axis, route)


def absorb(maxima, totals, targets, block_peak, block_total):
    raised = maxima.at[targets].max(block_peak)
    totals = totals * jnp.exp(maxima - raised)
    totals = totals.at[targets].add(block_total * jnp.exp(block_peak - raised[targets]))
    return (raised, totals)


def combine_stats(first_pair, second_pair):
    joined = jnp.maximum(first_pair[0], second_pair[0])
    merged_sum = first_pair[1] * jnp.exp(first_pair[0] - joined) + second_pair[1] * jnp.exp(
        second_pair[0] - joined
    )
    return (joined, merged_sum)


def blank(blocks, frames):
    return (
        jnp.full((blocks, frames), empty_peak, jnp.float32),
        jnp.zeros((blocks, frames), jnp.float32),
    )


def block_stats(
    local_side, far_side, potential, slot_plan, column, first_slot, final_position_entry, running
):
    slot_count = slot_plan.shape[0]

    def group(counter, current):
        maxima, totals = current
        slot_ids = first_slot + counter * slot_batch + lax.iota(jnp.int32, slot_batch)
        usable = slot_ids < final_position_entry
        slot_ids = jnp.minimum(slot_ids, slot_count - 1)
        near = slot_plan[slot_ids, column]
        distant = slot_plan[slot_ids, 1 - column]
        similarity_matrix = (
            jnp.einsum(
                "fdg,fwg->fdw",
                local_side[near],
                far_side[distant],
                preferred_element_type=jnp.float32,
            )
            / smoothing_epsilon
        )
        similarity_matrix = similarity_matrix + potential[distant][:, None, :]
        block_peak = jnp.max(similarity_matrix, axis=2)
        block_total = jnp.sum(jnp.exp(similarity_matrix - block_peak[:, :, None]), axis=2)
        block_peak = jnp.where(usable[:, None], block_peak, empty_peak)
        block_total = jnp.where(usable[:, None], block_total, 0.0)
        return absorb(maxima, totals, near, block_peak, block_total)

    groups = jnp.maximum(final_position_entry - first_slot + slot_batch - 1, 0) // slot_batch
    return lax.fori_loop(0, groups, group, running)


def fold_rows(running):
    peak_all = lax.pmax(running[0], "tgt")
    summed = lax.psum(running[1] * jnp.exp(running[0] - peak_all), "tgt")
    result = (peak_all, summed)
    return result


def collapse_columns(running):
    peak_all = lax.pmax(running[0], "src")
    summed = lax.psum(running[1] * jnp.exp(running[0] - peak_all), "src")
    result = (peak_all, summed)
    return result


def finish(log_mass, running):
    return log_mass - (running[0] + jnp.log(running[1]))


def on_device(
    source_embed, target_embed, source_mass, target_mass, target_start, block_pairs, counts
):
    source_full = lax.all_gather(source_embed, "tgt", axis=2, tiled=True)
    target_full = lax.all_gather(target_embed, "src", axis=2, tiled=True)
    slot_plan = block_pairs.reshape(block_pairs.shape[2], 2)
    live_count = counts.reshape(())
    source_blocks = source_full.shape[0]
    target_blocks = target_full.shape[0]
    frames = source_full.shape[1]
    target_dual_potential = target_start
    sender_log_scaling = source_mass
    halfway = lax.axis_size("src").bit_length() - 2
    partner_full = from_partner(source_full, "src", halfway)
    partner_plan, matched_block_number = from_partner((slot_plan, live_count), "src", halfway)
    shared = (live_count + matched_block_number + 1) // 2
    own_last = jnp.minimum(live_count, shared)
    lent_first = jnp.minimum(matched_block_number, shared)
    for iteration in range(ITERS):
        running = block_stats(
            source_full,
            target_full,
            target_dual_potential,
            slot_plan,
            0,
            0,
            own_last,
            blank(source_blocks, frames),
        )
        lent = block_stats(
            partner_full,
            target_full,
            target_dual_potential,
            partner_plan,
            0,
            lent_first,
            matched_block_number,
            blank(source_blocks, frames),
        )
        returned = from_partner((lent[0], lent[1]), "src", halfway)
        running = combine_stats(running, returned)
        sender_log_scaling = finish(source_mass, fold_rows(running))
        partner_pot = from_partner(sender_log_scaling, "src", halfway)
        running = block_stats(
            target_full,
            source_full,
            sender_log_scaling,
            slot_plan,
            1,
            0,
            own_last,
            blank(target_blocks, frames),
        )
        running = block_stats(
            target_full,
            partner_full,
            partner_pot,
            partner_plan,
            1,
            lent_first,
            matched_block_number,
            running,
        )
        target_dual_potential = finish(target_mass, collapse_columns(running))
    return (sender_log_scaling, target_dual_potential)


def solution(mesh):
    in_specs = (
        P("src", None, "tgt"),
        P("tgt", None, "src"),
        P("src", None),
        P("tgt", None),
        P("tgt", None),
        P("src", "tgt", None, None),
        P("src", "tgt"),
    )
    out_specs = (P("src", None), P("tgt", None))
    return jax.shard_map(
        on_device, mesh=mesh, in_specs=in_specs, out_specs=out_specs, check_vma=False
    )
```

profile of v0, /device:TPU:3, one launch (start us, length us, event | category | flops | bytes accessed | tf_op | source)
XLA Modules:
  0.0 464.4 jit_solution(17082557890183272998)
XLA Ops:
  0.6 1.0 copy.13
  1.6 8.0 %all_gather.6 = bf16[16,128,128]{1,0,2:T(8,128)(2,1)S(1)} all-gather(bf16[16,128,32]{1,0,2:T(8,128)(2,1)S(1)} %copy.13), channel_id=1, replica_groups=mesh['src'=8,'tgt'=4] {'tgt'}, dimensions={2}, use_global_device_ids=true | all-gather | bytes 655360 | tf_op jit(solution)/shard_map/all_gather | solution.py:97
  9.6 2.3 collective-permute-start.2
  12.6 1.7 collective-permute-start.1
  15.8 30.6 %all_gather.7 = bf16[16,128,128]{1,0,2:T(8,128)(2,1)S(1)} all-gather(bf16[16,128,16]{1,0,2:T(8,128)(2,1)S(1)} %copy.14), channel_id=1, replica_groups=mesh['src'=8,'tgt'=4] {'src'}, dimensions={2}, use_global_device_ids=true | all-gather | bytes 589824 | tf_op jit(solution)/shard_map/all_gather | solution.py:98
  49.5 0.7 copy-done.1
  50.5 2.0 collective-permute-start.4
  52.5 10.0 %while.96 = (s32[]{:T(128)}, f32[16,128]{1,0:T(8,128)S(1)}, f32[16,128]{1,0:T(8,128)S(1)}, s32[]{:T(128)}, s32[128,2]{0,1:T(2,128)S(1)}, /*index=5*/s32[]{:T(128...) while((s32[]{:T(128)}, f32[16,128]{1,0:T(8,128)S(1)}, ...), condition=%wide.region_5.6_spmd, body=%wide.region_0.5_spmd.sunk | while | flops 34221184 | bytes 2762505 | solution.py:73
  52.6 0.7 gather_fusion
  53.2 0.6 gather_fusion.3
  53.8 0.7 gather_fusion.1
  54.5 0.6 gather_fusion.4
  56.1 0.7 scatter_custom_fusion.66
  56.8 0.7 scatter_custom_fusion.67
  57.6 0.7 gather_fusion
  58.9 0.7 gather_fusion.1
  59.5 0.6 gather_fusion.4
  61.1 0.7 scatter_custom_fusion.66
  61.9 0.7 scatter_custom_fusion.67
  62.6 35.8 %pmax.28 = f32[16,128]{1,0:T(8,128)S(1)} all-reduce(f32[16,128]{1,0:T(8,128)S(1)} %max.44), channel_id=1, replica_groups=mesh['src'=8,'tgt'=4] {'tgt'}, use_global_device_ids=true, to_apply=%region_12.13 | all-reduce | flops 2048 | bytes 16384 | tf_op jit(solution)/shard_map/pmax | solution.py:77
  98.5 5.9 %psum.28 = f32[16,128]{1,0:T(8,128)S(1)} all-reduce(f32[16,128]{1,0:T(8,128)S(1)} %exponential_multiply_fusion.11), channel_id=1, replica_groups=mesh['src'=8,'tgt'=4] {'tgt'}, use_global_device_ids=true, to_apply=%region_13.14 | all-reduce | flops 2048 | bytes 16384 | tf_op jit(solution)/shard_map/psum | solution.py:78
  104.4 0.6 add_subtract_fusion.3
  105.0 8.7 %collective-permute-start.5 = (f32[16,128]{1,0:T(8,128)}, f32[16,128]{1,0:T(8,128)S(1)}, u32[]{:S(2)}, u32[]{:S(2)}) collective-permute-start(f32[16,128]{1,0:T(8,128)} %add_subtract_fusion.3), channel_id=1, source_target_pairs={{0,16},{16,0},{4,20},{20,4},{8,24},{24,8},{12,28},{28,12},{1,17},{... | collective-permute-start | bytes 24584 | tf_op jit(solution)/shard_map/ppermute | solution.py:19
  113.7 11.4 %while.98 = (s32[]{:T(128)}, f32[16,128]{1,0:T(8,128)S(1)}, f32[16,128]{1,0:T(8,128)S(1)}, s32[]{:T(128)}, s32[128,2]{0,1:T(2,128)S(1)}, /*index=5*/s32[]{:T(128...) while((s32[]{:T(128)}, f32[16,128]{1,0:T(8,128)S(1)}, ...), condition=%wide.region_19.20_spmd, body=%wide.region_14.19_spmd.sunk | while | flops 34221184 | bytes 2762505 | solution.py:73
  113.7 0.7 gather_fusion.10
  114.4 0.6 gather_fusion.13
  115.0 0.7 gather_fusion.11
  116.3 1.3 gather_fusion.12
  118.0 0.7 scatter_custom_fusion.74
  118.7 0.7 scatter_custom_fusion.75
  119.5 0.7 gather_fusion.10
  120.7 0.7 gather_fusion.11
  122.0 1.3 gather_fusion.12
  123.7 0.7 scatter_custom_fusion.74
  124.4 0.7 scatter_custom_fusion.75
  125.2 117.4 %pmax.29 = f32[16,128]{1,0:T(8,128)S(1)} all-reduce(f32[16,128]{1,0:T(8,128)S(1)} %get-tuple-element.420), channel_id=1, replica_groups=mesh['src'=8,'tgt'=4] {'src'}, use_global_device_ids=true, to_apply=%region_26.27 | all-reduce | flops 2048 | bytes 16384 | tf_op jit(solution)/shard_map/pmax | solution.py:84
  242.7 14.0 %psum.29 = f32[16,128]{1,0:T(8,128)S(1)} all-reduce(f32[16,128]{1,0:T(8,128)S(1)} %exponential_multiply_fusion.10), channel_id=1, replica_groups=mesh['src'=8,'tgt'=4] {'src'}, use_global_device_ids=true, to_apply=%region_27.28 | all-reduce | flops 2048 | bytes 16384 | tf_op jit(solution)/shard_map/psum | solution.py:85
  256.9 2.4 collective-permute-start.7
  259.2 10.0 %while.100 = (s32[]{:T(128)}, f32[16,128]{1,0:T(8,128)S(1)}, f32[16,128]{1,0:T(8,128)S(1)}, s32[]{:T(128)}, s32[128,2]{0,1:T(2,128)S(1)}, /*index=5*/s32[]{:T(12...) while((s32[]{:T(128)}, f32[16,128]{1,0:T(8,128)S(1)}, ...), condition=%wide.region_33.34_spmd, body=%wide.region_28.33_spmd.sunk | while | flops 34221184 | bytes 2762505 | solution.py:73
  259.2 0.7 gather_fusion.20
  260.5 0.7 gather_fusion.21
  262.8 0.7 scatter_custom_fusion.82
  263.5 0.7 scatter_custom_fusion.83
  264.2 0.7 gather_fusion.20
  265.5 0.7 gather_fusion.21
  267.8 0.7 scatter_custom_fusion.82
  268.5 0.7 scatter_custom_fusion.83
  269.3 25.2 %pmax.30 = f32[16,128]{1,0:T(8,128)S(1)} all-reduce(f32[16,128]{1,0:T(8,128)S(1)} %max.45), channel_id=1, replica_groups=mesh['src'=8,'tgt'=4] {'tgt'}, use_global_device_ids=true, to_apply=%region_40.41 | all-reduce | flops 2048 | bytes 16384 | tf_op jit(solution)/shard_map/pmax | solution.py:77
  294.5 5.9 %psum.30 = f32[16,128]{1,0:T(8,128)S(1)} all-reduce(f32[16,128]{1,0:T(8,128)S(1)} %exponential_multiply_fusion.9), channel_id=1, replica_groups=mesh['src'=8,'tgt'=4] {'tgt'}, use_global_device_ids=true, to_apply=%region_41.42 | all-reduce | flops 2048 | bytes 16384 | tf_op jit(solution)/shard_map/psum | solution.py:78
  300.4 0.6 add_subtract_fusion.1
  301.0 11.4 %while.102 = (s32[]{:T(128)}, f32[16,128]{1,0:T(8,128)S(1)}, f32[16,128]{1,0:T(8,128)S(1)}, s32[]{:T(128)}, s32[128,2]{0,1:T(2,128)S(1)}, /*index=5*/s32[]{:T(12...) while((s32[]{:T(128)}, f32[16,128]{1,0:T(8,128)S(1)}, ...), condition=%wide.region_47.48_spmd, body=%wide.region_42.47_spmd.sunk | while | flops 34221184 | bytes 2762505 | solution.py:73
  301.1 0.7 gather_fusion.30
  302.3 0.7 gather_fusion.31
  303.6 1.3 gather_fusion.32
  305.3 0.7 scatter_custom_fusion.90
  306.0 0.7 scatter_custom_fusion.91
  306.8 0.7 gather_fusion.30
  308.1 0.7 gather_fusion.31
  309.3 1.3 gather_fusion.32
  311.0 0.7 scatter_custom_fusion.90
  311.7 0.7 scatter_custom_fusion.91
  312.5 137.2 %pmax.31 = f32[16,128]{1,0:T(8,128)S(1)} all-reduce(f32[16,128]{1,0:T(8,128)S(1)} %get-tuple-element.428), channel_id=1, replica_groups=mesh['src'=8,'tgt'=4] {'src'}, use_global_device_ids=true, to_apply=%region_54.55 | all-reduce | flops 2048 | bytes 16384 | tf_op jit(solution)/shard_map/pmax | solution.py:84
  449.7 14.0 %psum.31 = f32[16,128]{1,0:T(8,128)S(1)} all-reduce(f32[16,128]{1,0:T(8,128)S(1)} %exponential_multiply_fusion.8), channel_id=1, replica_groups=mesh['src'=8,'tgt'=4] {'src'}, use_global_device_ids=true, to_apply=%region_55.56 | all-reduce | flops 2048 | bytes 16384 | tf_op jit(solution)/shard_map/psum | solution.py:85
  463.8 0.6 add_subtract_fusion
  (153 shorter events, 16.2 us)
Async XLA Ops:
  9.6 39.4 %collective-permute-start.2 = (bf16[16,128,128]{1,0,2:T(8,128)(2,1)S(1)}, bf16[16,128,128]{1,0,2:T(8,128)(2,1)S(1)}, u32[]{:S(2)}, u32[]{:S(2)}) collective-permute-start(bf16[16,128,128]{1,0,2:T(8,128)(2,1)S(1)} %all_gather.6), channel_id=1, source_target_pairs={{0,16},{16,0},{4,20},{20,4},{8,24},{24,8},{12,28},{28,12},{1,17},{... | collective-permute-start | bytes 1572872 | tf_op jit(solution)/shard_map/ppermute | solution.py:19
  11.9 0.7 copy-start
  11.9 34.9 %collective-permute-start = (s32[]{:T(128)}, s32[]{:T(128)}, u32[]{:S(2)}, u32[]{:S(2)}) collective-permute-start(s32[]{:T(128)} %bitcast.48), channel_id=1, source_target_pairs={{0,16},{16,0},{4,20},{20,4},{8,24},{24,8},{12,28},{28,12},{1,17},{... | collective-permute-start | bytes 20 | tf_op jit(solution)/shard_map/ppermute | solution.py:19
  12.6 36.9 %collective-permute-start.1 = (s32[128,2]{0,1:T(2,128)S(1)}, s32[128,2]{0,1:T(2,128)S(1)}, u32[]{:S(2)}, u32[]{:S(2)}) collective-permute-start(s32[128,2]{0,1:T(2,128)S(1)} %bitcast.228), channel_id=1, source_target_pairs={{0,16},{16,0},{4,20},{20,4},{8,24},{24,8},{12,28},{28,12},{1,17},{... | collective-permute-start | bytes 3080 | tf_op jit(solution)/shard_map/ppermute | solution.py:19
  14.9 0.8 copy-start.2
  49.5 0.7 copy-start.1
  50.2 12.4 %collective-permute-start.3 = (f32[16,128]{1,0:T(8,128)S(1)}, f32[16,128]{1,0:T(8,128)S(1)}, u32[]{:S(2)}, u32[]{:S(2)}) collective-permute-start(f32[16,128]{1,0:T(8,128)S(1)} %get-tuple-element.415), channel_id=1, source_target_pairs={{0,16},{16,0},{4,20},{20,4},{8,24},{24,8},{12,28},{28,12},{1,17},{... | collective-permute-start | bytes 24584 | tf_op jit(solution)/shard_map/ppermute | solution.py:19
  50.5 47.9 %collective-permute-start.4 = (f32[16,128]{1,0:T(8,128)S(1)}, f32[16,128]{1,0:T(8,128)S(1)}, u32[]{:S(2)}, u32[]{:S(2)}) collective-permute-start(f32[16,128]{1,0:T(8,128)S(1)} %get-tuple-element.417), channel_id=1, source_target_pairs={{0,16},{16,0},{4,20},{20,4},{8,24},{24,8},{12,28},{28,12},{1,17},{... | collective-permute-start | bytes 24584 | tf_op jit(solution)/shard_map/ppermute | solution.py:19
  98.5 5.9 %copy-start.3 = (f32[16,128]{1,0:T(8,128)S(1)}, f32[16,128]{1,0:T(8,128)}, u32[]{:S(2)}) copy-start(f32[16,128]{1,0:T(8,128)} %param.25) | copy-start | bytes 24580
  105.0 20.2 %collective-permute-start.5 = (f32[16,128]{1,0:T(8,128)}, f32[16,128]{1,0:T(8,128)S(1)}, u32[]{:S(2)}, u32[]{:S(2)}) collective-permute-start(f32[16,128]{1,0:T(8,128)} %add_subtract_fusion.3), channel_id=1, source_target_pairs={{0,16},{16,0},{4,20},{20,4},{8,24},{24,8},{12,28},{28,12},{1,17},{... | collective-permute-start | bytes 24584 | tf_op jit(solution)/shard_map/ppermute | solution.py:19
  242.7 14.1 %copy-start.4 = (f32[16,128]{1,0:T(8,128)S(1)}, f32[16,128]{1,0:T(8,128)}, u32[]{:S(2)}) copy-start(f32[16,128]{1,0:T(8,128)} %param.26) | copy-start | bytes 24580
  256.8 12.5 %collective-permute-start.6 = (f32[16,128]{1,0:T(8,128)S(1)}, f32[16,128]{1,0:T(8,128)S(1)}, u32[]{:S(2)}, u32[]{:S(2)}) collective-permute-start(f32[16,128]{1,0:T(8,128)S(1)} %get-tuple-element.423), channel_id=1, source_target_pairs={{0,16},{16,0},{4,20},{20,4},{8,24},{24,8},{12,28},{28,12},{1,17},{... | collective-permute-start | bytes 24584 | tf_op jit(solution)/shard_map/ppermute | solution.py:19
  256.9 37.6 %collective-permute-start.7 = (f32[16,128]{1,0:T(8,128)S(1)}, f32[16,128]{1,0:T(8,128)S(1)}, u32[]{:S(2)}, u32[]{:S(2)}) collective-permute-start(f32[16,128]{1,0:T(8,128)S(1)} %get-tuple-element.425), channel_id=1, source_target_pairs={{0,16},{16,0},{4,20},{20,4},{8,24},{24,8},{12,28},{28,12},{1,17},{... | collective-permute-start | bytes 24584 | tf_op jit(solution)/shard_map/ppermute | solution.py:19
  301.0 11.4 %collective-permute-start.8 = (f32[16,128]{1,0:T(8,128)}, f32[16,128]{1,0:T(8,128)S(1)}, u32[]{:S(2)}, u32[]{:S(2)}) collective-permute-start(f32[16,128]{1,0:T(8,128)} %add_subtract_fusion.1), channel_id=1, source_target_pairs={{0,16},{16,0},{4,20},{20,4},{8,24},{24,8},{12,28},{28,12},{1,17},{... | collective-permute-start | bytes 24584 | tf_op jit(solution)/shard_map/ppermute | solution.py:19
where the time goes:
time: 467 us; the launch traced here: 464 us
  blocking collectives  394 us (84%)
  local copies, waits for them, and re-layouts  31.4 us (7%)
  starting transfers between devices  17.6 us (4%)
  other arithmetic  14.1 us (3%)
    pmax x2, blocking collectives, collapse_columns(): peak_all = lax.pmax(running[0], 'src')  255 us
    pmax x2, blocking collectives, fold_rows(): peak_all = lax.pmax(running[0], 'tgt')  61 us
    all_gather x1, blocking collectives, on_device(): target_full = lax.all_gather(target_embed, 'src', axis=2, tiled=True)  30.6 us
    psum x2, blocking collectives, collapse_columns(): summed = lax.psum(running[1] * jnp.exp(running[0] - peak_all), 'src')  28.1 us
    ppermute x9, starting transfers between devices, from_partner(): return lax.ppermute(block, axis, route)  17.6 us
    psum x2, blocking collectives, fold_rows(): summed = lax.psum(running[1] * jnp.exp(running[0] - peak_all), 'tgt')  11.8 us
  transfers between devices with their start and end apart: 9, of which 0 were waited for; matrix products, arithmetic and copies ran while one was open for 9% of the time, Pallas kernels for 0%

commit v1 on v0

--- a/solution.py
+++ b/solution.py
@@ -7,6 +7,22 @@
 smoothing_epsilon = 4.0
 empty_peak = -1e30
 slot_batch = 8
+
+
+def gather_around(x, axis, dim):
+    ways, here, turn = (lax.axis_size(axis), lax.axis_index(axis), x.shape[dim])
+    dims = [n * ways if d == dim else n for d, n in enumerate(x.shape)]
+    full = lax.dynamic_update_slice_in_dim(jnp.zeros(dims, x.dtype), x, here * turn, axis=dim)
+    going_up = going_down = x
+    for far in range(1, ways // 2 + 1):
+        going_up = lax.ppermute(going_up, axis, [(d, (d + 1) % ways) for d in range(ways)])
+        full = lax.dynamic_update_slice_in_dim(full, going_up, (here - far) % ways * turn, axis=dim)
+        if 2 * far < ways:
+            going_down = lax.ppermute(going_down, axis, [(d, (d - 1) % ways) for d in range(ways)])
+            full = lax.dynamic_update_slice_in_dim(
+                full, going_down, (here + far) % ways * turn, axis=dim
+            )
+    return full
 
 
 def from_partner(block, axis, bit):
@@ -95,7 +111,7 @@
     source_embed, target_embed, source_mass, target_mass, target_start, block_pairs, counts
 ):
     source_full = lax.all_gather(source_embed, "tgt", axis=2, tiled=True)
-    target_full = lax.all_gather(target_embed, "src", axis=2, tiled=True)
+    target_full = gather_around(target_embed, "src", 2)
     slot_plan = block_pairs.reshape(block_pairs.shape[2], 2)
     live_count = counts.reshape(())
     source_blocks = source_full.shape[0]

time: 467 us -> 539 us (1.15)
  local copies, waits for them, and re-layouts: 31.4 us -> 74.2 us
  waiting for transfers between devices: 0.02 us -> 31.2 us
  blocking collectives: 394 us -> 370 us
  starting transfers between devices: 17.6 us -> 40.5 us
    dynamic_update_slice x0 -> x8, local copies, waits for them, and re-layouts: none -> 43.9 us  [the longest x4 20.4 us: gather_around(): lax.dynamic_update_slice_in_dim(full, going_up, (here - far) % ways * tur...]
    ppermute x0 -> x7, waiting for transfers between devices: none -> 31.2 us  [the longest x4 21.1 us: gather_around(): lax.ppermute(going_up, axis, [(d, (d + 1) % ways) for d in range(ways)])]
    all_gather x1 -> x0, blocking collectives: 30.6 us -> none  [on_device(): target_full = lax.all_gather(target_embed, 'src', axis=2, tiled=True)]
    ppermute x0 -> x7, starting transfers between devices: none -> 24.3 us  [the longest x4 23.2 us: gather_around(): lax.ppermute(going_up, axis, [(d, (d + 1) % ways) for d in range(ways)])]
  transfers between devices with their start and end apart: 9 -> 16, of which waited for: 0 -> 3; matrix products, arithmetic and copies ran while one was open for 9% -> 16% of each run, Pallas kernels for 0% -> 0%
where the time goes in v1:
time: 539 us; the launch traced here: 537 us
  blocking collectives  370 us (69%)
  local copies, waits for them, and re-layouts  74.2 us (14%)
  starting transfers between devices  40.5 us (8%)
  waiting for transfers between devices  31.2 us (6%)
  other arithmetic  14.1 us (3%)
    pmax x2, blocking collectives, collapse_columns(): peak_all = lax.pmax(running[0], 'src')  257 us
    pmax x2, blocking collectives, fold_rows(): peak_all = lax.pmax(running[0], 'tgt')  64.8 us
    psum x2, blocking collectives, collapse_columns(): summed = lax.psum(running[1] * jnp.exp(running[0] - peak_all), 'src')  28.1 us
    ppermute x4, starting transfers between devices, gather_around(): lax.ppermute(going_up, axis, [(d, (d + 1) % ways) for d in range(ways)])  23.2 us
    ppermute x4, waiting for transfers between devices, gather_around(): lax.ppermute(going_up, axis, [(d, (d + 1) % ways) for d in range(ways)])  21.1 us
    dynamic_update_slice x4, local copies, waits for them, and re-layouts, gather_around(): lax.dynamic_update_slice_in_dim(full, going_up, (here - far) % ways * tur...  20.4 us
    dynamic_update_slice x3, local copies, waits for them, and re-layouts, gather_around(): lax.dynamic_update_slice_in_dim(full, going_down, (here + far) % ways * t...  18.4 us
    ppermute x9, starting transfers between devices, from_partner(): return lax.ppermute(block, axis, route)  16.2 us
  transfers between devices with their start and end apart: 16, of which 3 were waited for; matrix products, arithmetic and copies ran while one was open for 16% of the time, Pallas kernels for 0%

profile of v1, /device:TPU:3, one launch (start us, length us, event | category | flops | bytes accessed | tf_op | source)
XLA Modules:
  0.0 536.7 jit_solution(4563557694879774276)
XLA Ops:
  0.6 1.0 copy.17
  1.6 8.2 %all_gather.3 = bf16[16,128,128]{1,0,2:T(8,128)(2,1)S(1)} all-gather(bf16[16,128,32]{1,0,2:T(8,128)(2,1)S(1)} %copy.17), channel_id=1, replica_groups=mesh['src'=8,'tgt'=4] {'tgt'}, dimensions={2}, use_global_device_ids=true | all-gather | bytes 655360 | tf_op jit(solution)/shard_map/all_gather | solution.py:113
  9.8 2.3 collective-permute-start.9
  12.4 4.2 collective-permute-start.1
  16.6 15.4 %collective-permute-done.1 = bf16[16,128,16]{2,1,0:T(8,128)(2,1)S(1)} collective-permute-done((bf16[16,128,16]{2,1,0:T(8,128)(2,1)S(1)}, bf16[16,128,16]{2,1,0:T(8,128)(2,1)S(1)}, u32[]{:S(2)}, u32[]{:S(2)}) %collective-permute-start.1) | collective-permute-done | bytes 65568 | tf_op jit(solution)/shard_map/ppermute | solution.py:18
  32.0 2.5 collective-permute-start.3
  34.5 1.2 collective-permute-start.4
  35.6 5.7 %collective-permute-done.3 = bf16[16,128,16]{2,1,0:T(8,128)(2,1)S(1)} collective-permute-done((bf16[16,128,16]{2,1,0:T(8,128)(2,1)S(1)}, bf16[16,128,16]{2,1,0:T(8,128)(2,1)S(1)}, u32[]{:S(2)}, u32[]{:S(2)}) %collective-permute-start.3) | collective-permute-done | bytes 65568 | tf_op jit(solution)/shard_map/ppermute | solution.py:18
  41.3 13.7 %collective-permute-start.5 = (bf16[16,128,16]{2,1,0:T(8,128)(2,1)S(1)}, bf16[16,128,16]{2,1,0:T(8,128)(2,1)}, u32[]{:S(2)}, u32[]{:S(2)}) collective-permute-start(bf16[16,128,16]{2,1,0:T(8,128)(2,1)S(1)} %collective-permute-done.3), channel_id=1, source_target_pairs={{0,4},{4,8},{8,12},{12,16},{16,20},{20,24},{24,28},{28,0},{1,5},{5... | collective-permute-start | bytes 196616 | tf_op jit(solution)/shard_map/ppermute | solution.py:18
  55.1 10.0 %collective-permute-done.4 = bf16[16,128,16]{2,1,0:T(8,128)(2,1)} collective-permute-done((bf16[16,128,16]{2,1,0:T(8,128)(2,1)S(1)}, bf16[16,128,16]{2,1,0:T(8,128)(2,1)}, u32[]{:S(2)}, u32[]{:S(2)}) %collective-permute-start.4) | collective-permute-done | bytes 65568 | tf_op jit(solution)/shard_map/ppermute | solution.py:21
  65.1 2.8 collective-permute-start.7
  67.9 1.8 collective-permute-start
  69.7 0.7 collective-permute-start.8
  71.6 5.1 dynamic_update_slice.24
  78.4 1.9 dynamic_update_slice.25
  80.4 5.1 dynamic_update_slice.26
  85.5 5.1 dynamic_update_slice.27
  90.6 6.7 %dynamic_update_slice.28 = bf16[16,128,128]{2,1,0:T(8,128)(2,1)S(1)} dynamic-update-slice(bf16[16,128,128]{2,1,0:T(8,128)(2,1)S(1)} %dynamic_update_slice.27, bf16[16,128,16]{2,1,0:T(8,128)(2,1)} %collective-permute-done.4, s32[]{:T(128)} %copy.143, s32[]{:T(128)} %copy.143, s32[]{:T(128)S(6)} %select_n.410) | dynamic-update-slice | bytes 131076 | tf_op jit(solution)/shard_map/dynamic_update_slice | solution.py:22
  97.2 6.7 %dynamic_update_slice.29 = bf16[16,128,128]{2,1,0:T(8,128)(2,1)S(1)} dynamic-update-slice(bf16[16,128,128]{2,1,0:T(8,128)(2,1)S(1)} %dynamic_update_slice.28, bf16[16,128,16]{2,1,0:T(8,128)(2,1)} %collective-permute-done.5, s32[]{:T(128)} %copy.143, s32[]{:T(128)} %copy.143, s32[]{:T(128)S(6)} %select_n.412) | dynamic-update-slice | bytes 131076 | tf_op jit(solution)/shard_map/dynamic_update_slice | solution.py:19
  103.9 6.7 %dynamic_update_slice.30 = bf16[16,128,128]{2,1,0:T(8,128)(2,1)S(1)} dynamic-update-slice(bf16[16,128,128]{2,1,0:T(8,128)(2,1)S(1)} %dynamic_update_slice.29, bf16[16,128,16]{2,1,0:T(8,128)(2,1)} %collective-permute-done.6, s32[]{:T(128)} %copy.143, s32[]{:T(128)} %copy.143, s32[]{:T(128)S(6)} %select_n.414) | dynamic-update-slice | bytes 131076 | tf_op jit(solution)/shard_map/dynamic_update_slice | solution.py:22
  110.6 6.7 %dynamic_update_slice.31 = bf16[16,128,128]{2,1,0:T(8,128)(2,1)S(1)} dynamic-update-slice(bf16[16,128,128]{2,1,0:T(8,128)(2,1)S(1)} %dynamic_update_slice.30, bf16[16,128,16]{2,1,0:T(8,128)(2,1)} %collective-permute-done.7, s32[]{:T(128)} %copy.143, s32[]{:T(128)} %copy.143, s32[]{:T(128)S(6)} %select_n.416) | dynamic-update-slice | bytes 131076 | tf_op jit(solution)/shard_map/dynamic_update_slice | solution.py:19
  117.9 0.7 copy-done.1
  118.5 2.9 collective-permute-start.10
  121.5 10.0 %while.96 = (s32[]{:T(128)}, f32[16,128]{1,0:T(8,128)S(1)}, f32[16,128]{1,0:T(8,128)S(1)}, s32[]{:T(128)}, s32[128,2]{0,1:T(2,128)S(1)}, /*index=5*/s32[]{:T(128...) while((s32[]{:T(128)}, f32[16,128]{1,0:T(8,128)S(1)}, ...), condition=%wide.region_5.6_spmd, body=%wide.region_0.5_spmd.sunk | while | flops 34221184 | bytes 2762505 | solution.py:89
  121.5 0.7 gather_fusion
  122.7 0.7 gather_fusion.1
  125.0 0.7 scatter_custom_fusion.66
  125.7 0.7 scatter_custom_fusion.67
  126.5 0.7 gather_fusion
  130.1 0.7 scatter_custom_fusion.66
  130.8 0.7 scatter_custom_fusion.67
  131.5 37.5 %pmax.28 = f32[16,128]{1,0:T(8,128)S(1)} all-reduce(f32[16,128]{1,0:T(8,128)S(1)} %max.44), channel_id=1, replica_groups=mesh['src'=8,'tgt'=4] {'tgt'}, use_global_device_ids=true, to_apply=%region_12.13 | all-reduce | flops 2048 | bytes 16384 | tf_op jit(solution)/shard_map/pmax | solution.py:93
  169.1 5.9 %psum.28 = f32[16,128]{1,0:T(8,128)S(1)} all-reduce(f32[16,128]{1,0:T(8,128)S(1)} %exponential_multiply_fusion.11), channel_id=1, replica_groups=mesh['src'=8,'tgt'=4] {'tgt'}, use_global_device_ids=true, to_apply=%region_13.14 | all-reduce | flops 2048 | bytes 16384 | tf_op jit(solution)/shard_map/psum | solution.py:94
  175.6 6.1 %collective-permute-start.12 = (f32[16,128]{1,0:T(8,128)}, f32[16,128]{1,0:T(8,128)S(1)}, u32[]{:S(2)}, u32[]{:S(2)}) collective-permute-start(f32[16,128]{1,0:T(8,128)} %add_subtract_fusion.3), channel_id=1, source_target_pairs={{0,16},{16,0},{4,20},{20,4},{8,24},{24,8},{12,28},{28,12},{1,17},{... | collective-permute-start | bytes 24584 | tf_op jit(solution)/shard_map/ppermute | solution.py:35
  181.6 11.4 %while.98 = (s32[]{:T(128)}, f32[16,128]{1,0:T(8,128)S(1)}, f32[16,128]{1,0:T(8,128)S(1)}, s32[]{:T(128)}, s32[128,2]{0,1:T(2,128)S(1)}, /*index=5*/s32[]{:T(128...) while((s32[]{:T(128)}, f32[16,128]{1,0:T(8,128)S(1)}, ...), condition=%wide.region_19.20_spmd, body=%wide.region_14.19_spmd.sunk | while | flops 34221184 | bytes 2762505 | solution.py:89
  181.6 0.7 gather_fusion.10
  182.9 0.7 gather_fusion.11
  184.2 1.3 gather_fusion.12
  185.9 0.7 scatter_custom_fusion.74
  186.6 0.7 scatter_custom_fusion.75
  187.4 0.7 gather_fusion.10
  188.6 0.7 gather_fusion.11
  189.9 1.3 gather_fusion.12
  191.6 0.7 scatter_custom_fusion.74
  192.3 0.7 scatter_custom_fusion.75
  193.3 123.4 %pmax.29 = f32[16,128]{1,0:T(8,128)S(1)} all-reduce(f32[16,128]{1,0:T(8,128)S(1)} %get-tuple-element.420), channel_id=1, replica_groups=mesh['src'=8,'tgt'=4] {'src'}, use_global_device_ids=true, to_apply=%region_26.27 | all-reduce | flops 2048 | bytes 16384 | tf_op jit(solution)/shard_map/pmax | solution.py:100
  316.7 14.0 %psum.29 = f32[16,128]{1,0:T(8,128)S(1)} all-reduce(f32[16,128]{1,0:T(8,128)S(1)} %exponential_multiply_fusion.10), channel_id=1, replica_groups=mesh['src'=8,'tgt'=4] {'src'}, use_global_device_ids=true, to_apply=%region_27.28 | all-reduce | flops 2048 | bytes 16384 | tf_op jit(solution)/shard_map/psum | solution.py:101
  330.9 2.4 collective-permute-start.14
  333.3 10.0 %while.100 = (s32[]{:T(128)}, f32[16,128]{1,0:T(8,128)S(1)}, f32[16,128]{1,0:T(8,128)S(1)}, s32[]{:T(128)}, s32[128,2]{0,1:T(2,128)S(1)}, /*index=5*/s32[]{:T(12...) while((s32[]{:T(128)}, f32[16,128]{1,0:T(8,128)S(1)}, ...), condition=%wide.region_33.34_spmd, body=%wide.region_28.33_spmd.sunk | while | flops 34221184 | bytes 2762505 | solution.py:89
  336.9 0.7 scatter_custom_fusion.82
  337.6 0.7 scatter_custom_fusion.83
  341.9 0.7 scatter_custom_fusion.82
  342.6 0.7 scatter_custom_fusion.83
  343.3 27.3 %pmax.30 = f32[16,128]{1,0:T(8,128)S(1)} all-reduce(f32[16,128]{1,0:T(8,128)S(1)} %max.45), channel_id=1, replica_groups=mesh['src'=8,'tgt'=4] {'tgt'}, use_global_device_ids=true, to_apply=%region_40.41 | all-reduce | flops 2048 | bytes 16384 | tf_op jit(solution)/shard_map/pmax | solution.py:93
  370.7 5.9 %psum.30 = f32[16,128]{1,0:T(8,128)S(1)} all-reduce(f32[16,128]{1,0:T(8,128)S(1)} %exponential_multiply_fusion.9), channel_id=1, replica_groups=mesh['src'=8,'tgt'=4] {'tgt'}, use_global_device_ids=true, to_apply=%region_41.42 | all-reduce | flops 2048 | bytes 16384 | tf_op jit(solution)/shard_map/psum | solution.py:94
  377.2 11.4 %while.102 = (s32[]{:T(128)}, f32[16,128]{1,0:T(8,128)S(1)}, f32[16,128]{1,0:T(8,128)S(1)}, s32[]{:T(128)}, s32[128,2]{0,1:T(2,128)S(1)}, /*index=5*/s32[]{:T(12...) while((s32[]{:T(128)}, f32[16,128]{1,0:T(8,128)S(1)}, ...), condition=%wide.region_47.48_spmd, body=%wide.region_42.47_spmd.sunk | while | flops 34221184 | bytes 2762505 | solution.py:89
  379.8 1.3 gather_fusion.32
  381.5 0.7 scatter_custom_fusion.90
  382.2 0.7 scatter_custom_fusion.91
  385.5 1.3 gather_fusion.32
  387.2 0.7 scatter_custom_fusion.90
  387.9 0.7 scatter_custom_fusion.91
  388.6 133.4 %pmax.31 = f32[16,128]{1,0:T(8,128)S(1)} all-reduce(f32[16,128]{1,0:T(8,128)S(1)} %get-tuple-element.428), channel_id=1, replica_groups=mesh['src'=8,'tgt'=4] {'src'}, use_global_device_ids=true, to_apply=%region_54.55 | all-reduce | flops 2048 | bytes 16384 | tf_op jit(solution)/shard_map/pmax | solution.py:100
  522.0 14.0 %psum.31 = f32[16,128]{1,0:T(8,128)S(1)} all-reduce(f32[16,128]{1,0:T(8,128)S(1)} %exponential_multiply_fusion.8), channel_id=1, replica_groups=mesh['src'=8,'tgt'=4] {'src'}, use_global_device_ids=true, to_apply=%region_55.56 | all-reduce | flops 2048 | bytes 16384 | tf_op jit(solution)/shard_map/psum | solution.py:101
  (182 shorter events, 25.1 us)
Async XLA Ops:
  1.6 10.5 %copy-start.6 = (bf16[16,128,16]{1,2,0:T(8,128)(2,1)S(1)}, bf16[16,128,16]{1,2,0:T(8,128)(2,1)}, u32[]{:S(2)}) copy-start(bf16[16,128,16]{1,2,0:T(8,128)(2,1)} %param.24) | copy-start | bytes 196612
  9.8 107.6 %collective-permute-start.9 = (bf16[16,128,128]{1,0,2:T(8,128)(2,1)S(1)}, bf16[16,128,128]{1,0,2:T(8,128)(2,1)S(1)}, u32[]{:S(2)}, u32[]{:S(2)}) collective-permute-start(bf16[16,128,128]{1,0,2:T(8,128)(2,1)S(1)} %all_gather.3), channel_id=1, source_target_pairs={{0,16},{16,0},{4,20},{20,4},{8,24},{24,8},{12,28},{28,12},{1,17},{... | collective-permute-start | bytes 1572872 | tf_op jit(solution)/shard_map/ppermute | solution.py:35
  12.4 19.6 %collective-permute-start.1 = (bf16[16,128,16]{2,1,0:T(8,128)(2,1)S(1)}, bf16[16,128,16]{2,1,0:T(8,128)(2,1)S(1)}, u32[]{:S(2)}, u32[]{:S(2)}) collective-permute-start(bf16[16,128,16]{2,1,0:T(8,128)(2,1)S(1)} %copy.18), channel_id=1, source_target_pairs={{0,4},{4,8},{8,12},{12,16},{16,20},{20,24},{24,28},{28,0},{1,5},{5... | collective-permute-start | bytes 196616 | tf_op jit(solution)/shard_map/ppermute | solution.py:18
  16.6 17.9 %collective-permute-start.2 = (bf16[16,128,16]{2,1,0:T(8,128)(2,1)S(1)}, bf16[16,128,16]{2,1,0:T(8,128)(2,1)S(1)}, u32[]{:S(2)}, u32[]{:S(2)}) collective-permute-start(bf16[16,128,16]{2,1,0:T(8,128)(2,1)S(1)} %copy.18), channel_id=1, source_target_pairs={{0,28},{4,0},{8,4},{12,8},{16,12},{20,16},{24,20},{28,24},{1,29},{... | collective-permute-start | bytes 196616 | tf_op jit(solution)/shard_map/ppermute | solution.py:21
  32.0 9.4 %collective-permute-start.3 = (bf16[16,128,16]{2,1,0:T(8,128)(2,1)S(1)}, bf16[16,128,16]{2,1,0:T(8,128)(2,1)S(1)}, u32[]{:S(2)}, u32[]{:S(2)}) collective-permute-start(bf16[16,128,16]{2,1,0:T(8,128)(2,1)S(1)} %collective-permute-done.1), channel_id=1, source_target_pairs={{0,4},{4,8},{8,12},{12,16},{16,20},{20,24},{24,28},{28,0},{1,5},{5... | collective-permute-start | bytes 196616 | tf_op jit(solution)/shard_map/ppermute | solution.py:18
  34.5 35.2 %copy-start.2 = (bf16[16,128,16]{2,1,0:T(8,128)(2,1)}, bf16[16,128,16]{2,1,0:T(8,128)(2,1)S(1)}, u32[]{:S(2)}) copy-start(bf16[16,128,16]{2,1,0:T(8,128)(2,1)S(1)} %collective-permute-done.2) | copy-start | bytes 196612
  34.5 30.6 %collective-permute-start.4 = (bf16[16,128,16]{2,1,0:T(8,128)(2,1)S(1)}, bf16[16,128,16]{2,1,0:T(8,128)(2,1)}, u32[]{:S(2)}, u32[]{:S(2)}) collective-permute-start(bf16[16,128,16]{2,1,0:T(8,128)(2,1)S(1)} %collective-permute-done.2), channel_id=1, source_target_pairs={{0,28},{4,0},{8,4},{12,8},{16,12},{20,16},{24,20},{28,24},{1,29},{... | collective-permute-start | bytes 196616 | tf_op jit(solution)/shard_map/ppermute | solution.py:21
  41.3 28.3 %copy-start.4 = (bf16[16,128,16]{2,1,0:T(8,128)(2,1)}, bf16[16,128,16]{2,1,0:T(8,128)(2,1)S(1)}, u32[]{:S(2)}) copy-start(bf16[16,128,16]{2,1,0:T(8,128)(2,1)S(1)} %collective-permute-done.3) | copy-start | bytes 196612
  41.3 23.8 %collective-permute-start.5 = (bf16[16,128,16]{2,1,0:T(8,128)(2,1)S(1)}, bf16[16,128,16]{2,1,0:T(8,128)(2,1)}, u32[]{:S(2)}, u32[]{:S(2)}) collective-permute-start(bf16[16,128,16]{2,1,0:T(8,128)(2,1)S(1)} %collective-permute-done.3), channel_id=1, source_target_pairs={{0,4},{4,8},{8,12},{12,16},{16,20},{20,24},{24,28},{28,0},{1,5},{5... | collective-permute-start | bytes 196616 | tf_op jit(solution)/shard_map/ppermute | solution.py:18
  65.1 38.8 %collective-permute-start.6 = (bf16[16,128,16]{2,1,0:T(8,128)(2,1)}, bf16[16,128,16]{2,1,0:T(8,128)(2,1)}, u32[]{:S(2)}, u32[]{:S(2)}) collective-permute-start(bf16[16,128,16]{2,1,0:T(8,128)(2,1)} %collective-permute-done.4), channel_id=1, source_target_pairs={{0,28},{4,0},{8,4},{12,8},{16,12},{20,16},{24,20},{28,24},{1,29},{... | collective-permute-start | bytes 196616 | tf_op jit(solution)/shard_map/ppermute | solution.py:21
  65.1 45.5 %collective-permute-start.7 = (bf16[16,128,16]{2,1,0:T(8,128)(2,1)}, bf16[16,128,16]{2,1,0:T(8,128)(2,1)}, u32[]{:S(2)}, u32[]{:S(2)}) collective-permute-start(bf16[16,128,16]{2,1,0:T(8,128)(2,1)} %collective-permute-done.5), channel_id=1, source_target_pairs={{0,4},{4,8},{8,12},{12,16},{16,20},{20,24},{24,28},{28,0},{1,5},{5... | collective-permute-start | bytes 196616 | tf_op jit(solution)/shard_map/ppermute | solution.py:18
  67.9 1.8 copy-start
  67.9 8.8 %collective-permute-start = (s32[]{:T(128)}, s32[]{:T(128)}, u32[]{:S(2)}, u32[]{:S(2)}) collective-permute-start(s32[]{:T(128)} %bitcast.48), channel_id=1, source_target_pairs={{0,16},{16,0},{4,20},{20,4},{8,24},{24,8},{12,28},{28,12},{1,17},{... | collective-permute-start | bytes 20 | tf_op jit(solution)/shard_map/ppermute | solution.py:35
  69.7 48.1 %collective-permute-start.8 = (s32[128,2]{0,1:T(2,128)S(1)}, s32[128,2]{0,1:T(2,128)S(1)}, u32[]{:S(2)}, u32[]{:S(2)}) collective-permute-start(s32[128,2]{0,1:T(2,128)S(1)} %bitcast.228), channel_id=1, source_target_pairs={{0,16},{16,0},{4,20},{20,4},{8,24},{24,8},{12,28},{28,12},{1,17},{... | collective-permute-start | bytes 3080 | tf_op jit(solution)/shard_map/ppermute | solution.py:35
  78.4 2.0 copy-start.3
  80.4 5.1 copy-start.5
  117.8 0.7 copy-start.1
  118.5 13.0 %collective-permute-start.10 = (f32[16,128]{1,0:T(8,128)S(1)}, f32[16,128]{1,0:T(8,128)S(1)}, u32[]{:S(2)}, u32[]{:S(2)}) collective-permute-start(f32[16,128]{1,0:T(8,128)S(1)} %get-tuple-element.415), channel_id=1, source_target_pairs={{0,16},{16,0},{4,20},{20,4},{8,24},{24,8},{12,28},{28,12},{1,17},{... | collective-permute-start | bytes 24584 | tf_op jit(solution)/shard_map/ppermute | solution.py:35
  121.4 47.6 %collective-permute-start.11 = (f32[16,128]{1,0:T(8,128)S(1)}, f32[16,128]{1,0:T(8,128)S(1)}, u32[]{:S(2)}, u32[]{:S(2)}) collective-permute-start(f32[16,128]{1,0:T(8,128)S(1)} %get-tuple-element.417), channel_id=1, source_target_pairs={{0,16},{16,0},{4,20},{20,4},{8,24},{24,8},{12,28},{28,12},{1,17},{... | collective-permute-start | bytes 24584 | tf_op jit(solution)/shard_map/ppermute | solution.py:35
  169.0 5.9 %copy-start.7 = (f32[16,128]{1,0:T(8,128)S(1)}, f32[16,128]{1,0:T(8,128)}, u32[]{:S(2)}) copy-start(f32[16,128]{1,0:T(8,128)} %param.25) | copy-start | bytes 24580
  175.6 17.5 %collective-permute-start.12 = (f32[16,128]{1,0:T(8,128)}, f32[16,128]{1,0:T(8,128)S(1)}, u32[]{:S(2)}, u32[]{:S(2)}) collective-permute-start(f32[16,128]{1,0:T(8,128)} %add_subtract_fusion.3), channel_id=1, source_target_pairs={{0,16},{16,0},{4,20},{20,4},{8,24},{24,8},{12,28},{28,12},{1,17},{... | collective-permute-start | bytes 24584 | tf_op jit(solution)/shard_map/ppermute | solution.py:35
  316.7 14.1 %copy-start.8 = (f32[16,128]{1,0:T(8,128)S(1)}, f32[16,128]{1,0:T(8,128)}, u32[]{:S(2)}) copy-start(f32[16,128]{1,0:T(8,128)} %param.26) | copy-start | bytes 24580
  330.8 12.5 %collective-permute-start.13 = (f32[16,128]{1,0:T(8,128)S(1)}, f32[16,128]{1,0:T(8,128)S(1)}, u32[]{:S(2)}, u32[]{:S(2)}) collective-permute-start(f32[16,128]{1,0:T(8,128)S(1)} %get-tuple-element.423), channel_id=1, source_target_pairs={{0,16},{16,0},{4,20},{20,4},{8,24},{24,8},{12,28},{28,12},{1,17},{... | collective-permute-start | bytes 24584 | tf_op jit(solution)/shard_map/ppermute | solution.py:35
  330.9 39.7 %collective-permute-start.14 = (f32[16,128]{1,0:T(8,128)S(1)}, f32[16,128]{1,0:T(8,128)S(1)}, u32[]{:S(2)}, u32[]{:S(2)}) collective-permute-start(f32[16,128]{1,0:T(8,128)S(1)} %get-tuple-element.425), channel_id=1, source_target_pairs={{0,16},{16,0},{4,20},{20,4},{8,24},{24,8},{12,28},{28,12},{1,17},{... | collective-permute-start | bytes 24584 | tf_op jit(solution)/shard_map/ppermute | solution.py:35
  377.2 11.4 %collective-permute-start.15 = (f32[16,128]{1,0:T(8,128)}, f32[16,128]{1,0:T(8,128)S(1)}, u32[]{:S(2)}, u32[]{:S(2)}) collective-permute-start(f32[16,128]{1,0:T(8,128)} %add_subtract_fusion.1), channel_id=1, source_target_pairs={{0,16},{16,0},{4,20},{20,4},{8,24},{24,8},{12,28},{28,12},{1,17},{... | collective-permute-start | bytes 24584 | tf_op jit(solution)/shard_map/ppermute | solution.py:35
